TPU v7x, 16 devices: a 4x2x1 block of a 4x4x8 slice. The times are simulated.
16 devices in a mesh: req: 2 (over y, z), cp: 8 (over x, core).
Axes of the slice: x: 4, y: 2, z: 1, core: 2. Of those that a mesh axis runs over, the one named last changes fastest.
The devices are a block of a 4x4x8 slice.
Arguments:
- hidden: bfloat16 [8192, 2048], P(('req', 'cp')), parts along dimension 0
- positions: int32 [8192], P(('req', 'cp')), parts along dimension 0
- gain_attn: bfloat16 [2, 2048], replicated
- gain_mlp: bfloat16 [2, 2048], replicated
- w_query: bfloat16 [2, 2048, 16, 128], replicated
- w_key: bfloat16 [2, 2048, 16, 128], replicated
- w_value: bfloat16 [2, 2048, 16, 128], replicated
- w_out: bfloat16 [2, 16, 128, 2048], replicated
- w_gate: bfloat16 [2, 2048, 8192], replicated
- w_up: bfloat16 [2, 2048, 8192], replicated
- w_down: bfloat16 [2, 8192, 2048], replicated
Outputs:
- output 1: bfloat16 [8192, 2048], P(('req', 'cp')), parts along dimension 0
- output 2: bfloat16 [2, 8192, 16, 128], P(None, 'req', 'cp'), parts along dimension 1
- output 3: bfloat16 [2, 8192, 16, 128], P(None, 'req', 'cp'), parts along dimension 1
There are 2 independent parts. A program takes and returns all parts, laid end to end along the dimension named above; an argument that names none is the same for every part.
All inputs are finite; a program needn't handle non-finite values.
Results may differ from a plain program's by a relative error of at most 0.016795.
Values are sent between devices in bfloat16 or wider.
A program may use at most 768 MiB of HBM per device.

v0:
```python
import jax
import jax.numpy as jnp
from jax import lax
from jax.sharding import PartitionSpec as P

NORM_EPS = 1e-5
ROPE_BASE = 10000.0


def rms_norm(values, gain_vec):
    wide_vals = values.astype(jnp.float32)
    inv_rms = lax.rsqrt(jnp.mean(wide_vals * wide_vals, axis=-1, keepdims=True) + NORM_EPS)
    return (wide_vals * inv_rms * gain_vec.astype(jnp.float32)).astype(jnp.bfloat16)


def rope_tables(pos_vec, head_dim):
    inv_freq = ROPE_BASE ** (-jnp.arange(0, head_dim, 2, dtype=jnp.float32) / head_dim)
    angles = pos_vec.astype(jnp.float32)[..., None] * inv_freq
    return jnp.cos(angles)[..., None, :], jnp.sin(angles)[..., None, :]


def rotate_half(values, cos_tab, sin_tab):
    half_dim = values.shape[-1] // 2
    lower_half = values[..., :half_dim]
    upper_half = values[..., half_dim:]
    return jnp.concatenate([lower_half * cos_tab - upper_half * sin_tab, upper_half * cos_tab + lower_half * sin_tab], axis=-1)


def to_natural(rows, cp_size):
    lead_dim = rows.shape[0]
    seq_len = rows.shape[1]
    split_rows = rows.reshape((lead_dim, cp_size, 2, seq_len // (2 * cp_size)) + rows.shape[2:])
    natural = jnp.concatenate([split_rows[:, :, 0], split_rows[:, ::-1, 1]], axis=1)
    return natural.reshape(rows.shape)


def attend(queries, key_all, value_all, pos_local, pos_all):
    num_tok = queries.shape[0]
    num_heads = queries.shape[1]
    head_dim = queries.shape[2]
    kv_heads = key_all.shape[1]
    grouped = queries.reshape(num_tok, kv_heads, num_heads // kv_heads, head_dim)
    scores = jnp.einsum("tkgd,skd->kgts", grouped, key_all, preferred_element_type=jnp.float32) * (head_dim ** -0.5)
    allowed = pos_all[None, :] <= pos_local[:, None]
    scores = jnp.where(allowed, scores, -jnp.inf)
    row_max = jnp.max(scores, axis=-1, keepdims=True)
    exp_scores = jnp.exp(scores - row_max)
    attn_probs = (exp_scores / jnp.sum(exp_scores, axis=-1, keepdims=True)).astype(jnp.bfloat16)
    attn_out = jnp.einsum("kgts,skd->tkgd", attn_probs, value_all, preferred_element_type=jnp.float32)
    return attn_out.astype(jnp.bfloat16).reshape(num_tok, num_heads, head_dim)


def solution(mesh):
    cp_size = mesh.shape["cp"]
    row_spec = P(("req", "cp"), None)
    pos_spec = P(("req", "cp"))
    rep_spec = P()
    cache_spec = P(None, "req", "cp", None)

    def per_device(hidden, positions, gain_attn, gain_mlp, w_query, w_key, w_value, w_out, w_gate, w_up, w_down):
        num_layers = w_query.shape[0]
        head_dim = w_query.shape[3]
        cos_tab, sin_tab = rope_tables(positions, head_dim)
        pos_all = lax.all_gather(positions, "cp", tiled=True)
        key_list = []
        value_list = []
        for layer_idx in range(num_layers):
            normed = rms_norm(hidden, gain_attn[layer_idx])
            q_proj = jnp.einsum("td,dhe->the", normed, w_query[layer_idx], preferred_element_type=jnp.float32)
            queries = rotate_half(q_proj, cos_tab, sin_tab).astype(jnp.bfloat16)
            k_proj = jnp.einsum("td,dhe->the", normed, w_key[layer_idx], preferred_element_type=jnp.float32)
            key_local = rotate_half(k_proj, cos_tab, sin_tab).astype(jnp.bfloat16)
            value_local = jnp.einsum("td,dhe->the", normed, w_value[layer_idx], preferred_element_type=jnp.float32).astype(jnp.bfloat16)
            key_all = lax.all_gather(key_local, "cp", tiled=True)
            value_all = lax.all_gather(value_local, "cp", tiled=True)
            attn_out = attend(queries, key_all, value_all, positions, pos_all)
            attn_proj = jnp.einsum("the,hed->td", attn_out, w_out[layer_idx], preferred_element_type=jnp.float32)
            hidden = (hidden.astype(jnp.float32) + attn_proj).astype(jnp.bfloat16)
            normed_mlp = rms_norm(hidden, gain_mlp[layer_idx])
            gate_act = jnp.dot(normed_mlp, w_gate[layer_idx], preferred_element_type=jnp.float32)
            up_act = jnp.dot(normed_mlp, w_up[layer_idx], preferred_element_type=jnp.float32)
            mlp_hidden = (jax.nn.silu(gate_act) * up_act).astype(jnp.bfloat16)
            mlp_out = jnp.dot(mlp_hidden, w_down[layer_idx], preferred_element_type=jnp.float32)
            hidden = (hidden.astype(jnp.float32) + mlp_out).astype(jnp.bfloat16)
            key_list.append(key_local)
            value_list.append(value_local)
        key_heads = lax.all_to_all(jnp.stack(key_list), "cp", 2, 1, tiled=True)
        value_heads = lax.all_to_all(jnp.stack(value_list), "cp", 2, 1, tiled=True)
        return hidden, to_natural(key_heads, cp_size), to_natural(value_heads, cp_size)

    in_specs = (row_spec, pos_spec, rep_spec, rep_spec, rep_spec, rep_spec, rep_spec, rep_spec, rep_spec, rep_spec, rep_spec)
    return jax.shard_map(per_device, mesh=mesh, in_specs=in_specs, out_specs=(row_spec, cache_spec, cache_spec), check_vma=False)
```

profile of v0, /device:TPU:113, one launch (start us, length us, event | category | flops | bytes accessed | tf_op | source)
XLA Modules:
  0.0 910.4 jit_solution(10391631986682979786)
XLA Ops:
  8.6 2.1 fusion.44
  10.7 12.2 %fusion.122 = (bf16[1,2048,16,128]{3,2,1,0:T(8,128)(2,1)}, bf16[1,2048,16,128]{3,2,1,0:T(8,128)(2,1)}) fusion(bf16[2,2048,16,128]{3,2,1,0:T(8,128)(2,1)} %param.15), kind=kLoop, calls=%fused_computation.135 | loop fusion | bytes 33554432 | tf_op jit(solution)/shard_map/slice | solution.py:69
  22.9 12.3 %copy.68 = bf16[1,2048,16,128]{1,3,2,0:T(8,128)(2,1)} copy(bf16[1,2048,16,128]{3,2,1,0:T(8,128)(2,1)} %get-tuple-element.4) | data formatting | bytes 16777216
  35.2 12.2 %fusion.123 = (bf16[1,2048,16,128]{3,2,1,0:T(8,128)(2,1)}, bf16[1,2048,16,128]{3,2,1,0:T(8,128)(2,1)}) fusion(bf16[2,2048,16,128]{3,2,1,0:T(8,128)(2,1)} %param.16), kind=kLoop, calls=%fused_computation.136 | loop fusion | bytes 33554432 | tf_op jit(solution)/shard_map/slice | solution.py:71
  47.4 12.4 %copy.67 = bf16[1,2048,16,128]{1,3,2,0:T(8,128)(2,1)} copy(bf16[1,2048,16,128]{3,2,1,0:T(8,128)(2,1)} %get-tuple-element.6) | data formatting | bytes 16777216
  59.8 7.3 fusion.117
  67.1 4.8 fusion.119
  72.5 2.5 subtract_convert_fusion.2
  78.1 10.0 %fusion.124 = (bf16[1,2048,16,128]{3,2,1,0:T(8,128)(2,1)}, bf16[1,2048,16,128]{3,2,1,0:T(8,128)(2,1)S(1)}) fusion(bf16[2,2048,16,128]{3,2,1,0:T(8,128)(2,1)} %param.17), kind=kLoop, calls=%fused_computation.137 | loop fusion | bytes 33554432 | tf_op jit(solution)/shard_map/slice | solution.py:73
  88.2 7.3 fusion.98
  95.6 12.4 %copy.70 = bf16[1,2048,16,128]{1,3,2,0:T(8,128)(2,1)} copy(bf16[1,2048,16,128]{3,2,1,0:T(8,128)(2,1)} %get-tuple-element.5) | data formatting | bytes 16777216
  108.0 12.4 %copy.71 = bf16[1,2048,16,128]{1,3,2,0:T(8,128)(2,1)} copy(bf16[1,2048,16,128]{3,2,1,0:T(8,128)(2,1)} %get-tuple-element.3) | data formatting | bytes 16777216
  120.4 21.4 %all-gather = s32[8,1,512]{2,1,0:T(1,128)S(1)} all-gather(s32[1,1,512]{2,1,0:T(1,128)S(1)} %bitcast.283), channel_id=1, replica_groups=mesh['req'=2,'cp'=8] {'cp'}, dimensions={0}, use_global_device_ids=true | all-gather | bytes 18432 | tf_op jit(solution)/shard_map/all_gather | solution.py:64
  144.4 18.2 %all-gather.8.cloned.1.call-done = bf16[4096,16,128]{0,2,1:T(8,128)(2,1)} async-done(((bf16[512,16,128]{0,2,1:T(8,128)(2,1)}), bf16[4096,16,128]{0,2,1:T(8,128)(2,1)}) %all-gather.8.cloned.1.call-update) | async-done | bytes 16777232 | tf_op jit(solution)/shard_map/all_gather | solution.py:74
  162.6 51.2 %fusion.2 = (f32[16,512]{1,0:T(8,128)S(1)}, f32[16,4096,512]{2,1,0:T(8,128)}) fusion(pred[512,4096]{0,1:T(8,128)(4,1)S(1)} %broadcast_compare_fusion, bf16[4096,16,128]{0,2,1:T(8,128)(2,1)} %all-gather.8.cloned.1.call-done, bf16[512,16,64]{0,2,1:T(8,128)(2,1)} %get-tuple-element.14, bf16[512,16,64]{0,2,1:T(8,128)(2,1)S(1)} %get-tuple-element.13), kind=kOutput, calls=%fused_computation.8 | convolution fusion | flops 8694784000 | bytes 155222016 | tf_op jit(solution)/shard_map/tkgd,skd->kgts/dot_general | solution.py:43
  213.8 41.1 %fusion = f32[16,512]{1,0:T(8,128)S(1)} fusion(f32[16,4096,512]{2,1,0:T(8,128)} %get-tuple-element.32, f32[16,512]{1,0:T(8,128)S(1)} %get-tuple-element.31, pred[512,4096]{0,1:T(8,128)(4,1)S(1)} %broadcast_compare_fusion), kind=kLoop, calls=%fused_computation.6 | loop fusion | flops 134209536 | bytes 136380416 | tf_op jit(solution)/shard_map/reduce_sum | solution.py:48
  254.9 52.8 %fusion.81.clone.5 = bf16[512,16,128]{0,2,1:T(8,128)(2,1)} fusion(f32[16,512]{1,0:T(8,128)S(1)} %fusion, f32[16,512]{1,0:T(8,128)S(1)} %get-tuple-element.31, f32[16,4096,512]{2,1,0:T(8,128)} %get-tuple-element.32, pred[512,4096]{0,1:T(8,128)(4,1)S(1)} %broadcast_compare_fusion, bf16[4096,16,128]{2,0,1:T(8,128)(2,1)} %all-gather.6.cloned.1.call-done), kind=kOutput, calls=%fused_computation.91.clone.clone.clone.2 | convolution fusion | flops 8757706752 | bytes 155254784 | tf_op jit(solution)/shard_map/kgts,skd->tkgd/dot_general | solution.py:49
  307.7 9.6 %fusion.48 = (f32[512]{0:T(512)S(1)}, bf16[512,2048]{1,0:T(8,128)(2,1)S(1)}) fusion(bf16[2,16,128,2048]{3,2,1,0:T(8,128)(2,1)} %param.18, bf16[512,2048]{1,0:T(8,128)(2,1)} %param.11, bf16[512,16,128]{0,2,1:T(8,128)(2,1)} %fusion.81.clone.5), kind=kOutput, calls=%fused_computation.62 | convolution fusion | flops 4301258240 | bytes 14682112 | tf_op jit(solution)/shard_map/the,hed->td/dot_general | solution.py:77
  317.3 25.2 %fusion.18 = f32[512,8192]{1,0:T(8,128)} fusion(bf16[2,2048,8192]{2,1,0:T(8,128)(2,1)} %param.19, bf16[512,2048]{1,0:T(8,128)(2,1)S(1)} %get-tuple-element.34, f32[2048]{0:T(1024)S(1)} %bitcast.292, f32[512]{0:T(512)S(1)} %add_rsqrt_fusion.2), kind=kOutput, calls=%fused_computation.24 | convolution fusion | flops 17184063488 | bytes 52439040 | tf_op jit(solution)/shard_map/dot_general | solution.py:80
  342.5 26.8 %multiply_convert_fusion.1.clone.3.clone.5 = bf16[512,8192]{1,0:T(8,128)(2,1)} fusion(f32[512,8192]{1,0:T(8,128)} %fusion.18, bf16[2,2048,8192]{2,1,0:T(8,128)(2,1)} %param.20, bf16[512,2048]{1,0:T(8,128)(2,1)S(1)} %get-tuple-element.34, f32[2048]{0:T(1024)S(1)} %bitcast.293, f32[512]{0:T(512)S(1)} %add_rsqrt_fusion.2), kind=kOutput, calls=%fused_computation.33.clone.clone.clone.clone.clone.clone.clone.2 | convolution fusion | flops 17209229312 | bytes 60827648 | tf_op jit(solution)/shard_map/dot_general | solution.py:81
  369.2 24.1 %fusion.52 = (f32[512]{0:T(512)S(1)}, bf16[512,2048]{1,0:T(8,128)(2,1)S(1)}) fusion(bf16[2,8192,2048]{2,1,0:T(8,128)(2,1)} %param.21, bf16[512,2048]{1,0:T(8,128)(2,1)S(1)} %get-tuple-element.34, bf16[512,8192]{1,0:T(8,128)(2,1)} %multiply_convert_fusion.1.clone.3.clone.5), kind=kOutput, calls=%fused_computation.66 | convolution fusion | flops 17186160640 | bytes 46139392 | tf_op jit(solution)/shard_map/dot_general | solution.py:83
  393.4 7.9 fusion.114
  401.3 7.2 fusion.112
  408.5 2.9 subtract_convert_fusion
  414.2 10.1 %fusion.101 = bf16[512,16,128]{2,0,1:T(8,128)(2,1)} fusion(bf16[1,2048,16,128]{3,2,1,0:T(8,128)(2,1)} %get-tuple-element.7, bf16[512,2048]{1,0:T(8,128)(2,1)} %copy-done.22, f32[2048]{0:T(1024)S(1)} %bitcast.288, f32[512]{0:T(512)S(1)} %add_rsqrt_fusion.1), kind=kOutput, calls=%fused_computation.111 | convolution fusion | flops 4300210176 | bytes 12593152 | tf_op jit(solution)/shard_map/td,dhe->the/dot_general | solution.py:73
  426.3 2.3 copy.53
  428.6 4.8 all-to-all-start.1
  435.0 2.5 copy.50
  437.5 89.5 %all-to-all-done.1 = bf16[2,512,16,128]{3,1,0,2:T(8,128)(2,1)} async-done(((bf16[2,512,16,128]{3,1,0,2:T(8,128)(2,1)}), bf16[2,512,16,128]{3,1,0,2:T(8,128)(2,1)}, u32[]{:S(2)}, u32[]{:S(2)}) %all-to-all-start.1) | async-done | bytes 4194336 | tf_op jit(solution)/shard_map/all_to_all | solution.py:88
  527.0 5.3 all-to-all-start
  532.3 3.9 fusion.125
  536.2 3.5 copy.75
  539.7 67.2 %all-to-all-done = bf16[2,512,16,128]{1,3,0,2:T(8,128)(2,1)} async-done(((bf16[2,512,16,128]{1,3,0,2:T(8,128)(2,1)}), bf16[2,512,16,128]{1,3,0,2:T(8,128)(2,1)}, u32[]{:S(2)}, u32[]{:S(2)}) %all-to-all-start) | async-done | bytes 4194336 | tf_op jit(solution)/shard_map/all_to_all | solution.py:87
  606.9 6.9 reshape.230
  613.8 10.0 %fusion.126 = (bf16[2,8,1,256,2,128]{3,2,5,0,4,1:T(2,128)(2,1)}, bf16[2,8,1,256,2,128]{3,2,5,0,4,1:T(2,128)(2,1)}) fusion(bf16[2,8,2,256,2,128]{3,2,5,0,4,1:T(2,128)(2,1)} %reshape.230), kind=kLoop, calls=%fused_computation.139 | loop fusion | bytes 8388608 | tf_op jit(solution)/shard_map/slice | solution.py:33
  623.8 9.4 %copy.73 = bf16[2,8,1,256,2,128]{5,4,3,1,0,2:T(2,128)(2,1)S(1)} copy(bf16[2,8,1,256,2,128]{3,2,5,0,4,1:T(2,128)(2,1)} %get-tuple-element.20) | data formatting | bytes 4194304
  633.2 11.2 %copy.72 = bf16[2,8,1,256,2,128]{5,4,3,1,0,2:T(2,128)(2,1)} copy(bf16[2,8,1,256,2,128]{3,2,5,0,4,1:T(2,128)(2,1)} %get-tuple-element.19) | data formatting | bytes 4194304
  644.4 2.9 reverse_bitcast_fusion.1
  647.3 6.0 copy_bitcast_fusion.4
  653.3 9.0 pad_maximum_fusion.2
  662.3 9.9 %pad_maximum_fusion = bf16[2,16,256,2,128]{4,3,2,1,0:T(2,128)(2,1)} fusion(bf16[2,8,256,2,128]{4,3,2,1,0:T(2,128)(2,1)} %reverse_bitcast_fusion.1, bf16[2,8,256,2,128]{4,3,2,1,0:T(2,128)(2,1)} %bitcast.273), kind=kLoop, calls=%fused_computation.75 | loop fusion | flops 2097152 | bytes 8388608 | tf_op jit(solution)/shard_map/concatenate | solution.py:33
  672.2 51.2 %fusion.3 = (f32[16,512]{1,0:T(8,128)S(1)}, f32[16,4096,512]{2,1,0:T(8,128)}) fusion(pred[512,4096]{0,1:T(8,128)(4,1)S(1)} %copy-done.1, bf16[4096,16,128]{0,2,1:T(8,128)(2,1)} %all-gather.12.cloned.1.call-done, bf16[512,16,64]{0,2,1:T(8,128)(2,1)} %get-tuple-element.10, bf16[512,16,64]{0,2,1:T(8,128)(2,1)S(1)} %copy-done.16), kind=kOutput, calls=%fused_computation.9 | convolution fusion | flops 8694784000 | bytes 155222016 | tf_op jit(solution)/shard_map/tkgd,skd->kgts/dot_general | solution.py:43
  723.4 41.1 %fusion.1 = f32[16,512]{1,0:T(8,128)S(1)} fusion(f32[16,4096,512]{2,1,0:T(8,128)} %get-tuple-element.38, f32[16,512]{1,0:T(8,128)S(1)} %get-tuple-element.37, pred[512,4096]{0,1:T(8,128)(4,1)S(1)} %copy-done.1), kind=kLoop, calls=%fused_computation.7 | loop fusion | flops 134209536 | bytes 136380416 | tf_op jit(solution)/shard_map/reduce_sum | solution.py:48
  764.5 52.7 %fusion.80.clone.5 = bf16[512,16,128]{0,2,1:T(8,128)(2,1)} fusion(f32[16,512]{1,0:T(8,128)S(1)} %fusion.1, f32[16,512]{1,0:T(8,128)S(1)} %get-tuple-element.37, f32[16,4096,512]{2,1,0:T(8,128)} %get-tuple-element.38, pred[512,4096]{0,1:T(8,128)(4,1)S(1)} %copy-done.1, bf16[4096,16,128]{2,0,1:T(8,128)(2,1)} %all-gather.10.cloned.1.call-done), kind=kOutput, calls=%fused_computation.90.clone.clone.clone.2 | convolution fusion | flops 8757706752 | bytes 155254784 | tf_op jit(solution)/shard_map/kgts,skd->tkgd/dot_general | solution.py:49
  817.2 9.6 %fusion.56 = (f32[512]{0:T(512)S(1)}, bf16[512,2048]{1,0:T(8,128)(2,1)S(1)}) fusion(bf16[2,16,128,2048]{3,2,1,0:T(8,128)(2,1)} %param.18, bf16[512,2048]{1,0:T(8,128)(2,1)} %copy-done.22, bf16[512,16,128]{0,2,1:T(8,128)(2,1)} %fusion.80.clone.5), kind=kOutput, calls=%fused_computation.70 | convolution fusion | flops 4301258240 | bytes 14682112 | tf_op jit(solution)/shard_map/the,hed->td/dot_general | solution.py:77
  826.8 25.4 %fusion.12 = f32[512,8192]{1,0:T(8,128)} fusion(bf16[2,2048,8192]{2,1,0:T(8,128)(2,1)} %param.19, bf16[512,2048]{1,0:T(8,128)(2,1)S(1)} %get-tuple-element.40, f32[2048]{0:T(1024)S(1)} %bitcast.284, f32[512]{0:T(512)S(1)} %add_rsqrt_fusion), kind=kOutput, calls=%fused_computation.18 | convolution fusion | flops 17184063488 | bytes 52439040 | tf_op jit(solution)/shard_map/dot_general | solution.py:80
  852.2 26.6 %multiply_convert_fusion.clone.7 = bf16[512,8192]{1,0:T(8,128)(2,1)} fusion(f32[512,8192]{1,0:T(8,128)} %fusion.12, bf16[2,2048,8192]{2,1,0:T(8,128)(2,1)} %param.20, bf16[512,2048]{1,0:T(8,128)(2,1)S(1)} %get-tuple-element.40, f32[2048]{0:T(1024)S(1)} %bitcast.285, f32[512]{0:T(512)S(1)} %add_rsqrt_fusion), kind=kOutput, calls=%fused_computation.32.clone.clone.clone.clone.clone.2 | convolution fusion | flops 17209229312 | bytes 60827648 | tf_op jit(solution)/shard_map/dot_general | solution.py:81
  878.8 24.6 %fusion.59 = bf16[512,2048]{1,0:T(8,128)(2,1)} fusion(bf16[512,2048]{1,0:T(8,128)(2,1)S(1)} %get-tuple-element.40, bf16[2,8192,2048]{2,1,0:T(8,128)(2,1)} %param.21, bf16[512,8192]{1,0:T(8,128)(2,1)} %multiply_convert_fusion.clone.7), kind=kOutput, calls=%fused_computation.73 | convolution fusion | flops 17183014912 | bytes 46137344 | tf_op jit(solution)/shard_map/dot_general | solution.py:83
  (71 shorter events, 14.3 us)
Async XLA Ops:
  7.2 155.4 %all-gather.8.cloned.1.call-start = ((), (), s32[]{:S(2)}) async-start(), calls=%async_computation.3 | async-start | bytes 18874368 | tf_op jit(solution)/shard_map/all_gather | solution.py:74
  47.4 12.4 %copy-start.11 = (bf16[512,2048]{1,0:T(8,128)(2,1)S(1)}, bf16[512,2048]{1,0:T(8,128)(2,1)}, u32[]{:S(2)}) copy-start(bf16[512,2048]{1,0:T(8,128)(2,1)} %param.11) | copy-start | bytes 6291460
  59.8 7.3 copy-start.7
  67.1 4.9 copy-start.18
  72.5 2.5 copy-start.12
  72.5 2.5 copy-start.14
  75.0 1.0 copy-start.2
  75.0 1.3 copy-start.4
  77.9 177.0 %all-gather.6.cloned.1.call-start = ((), (), s32[]{:S(2)}) async-start(), calls=%async_computation.2 | async-start | bytes 18874368 | tf_op jit(solution)/shard_map/all_gather | solution.py:75
  95.5 576.7 %all-gather.12.cloned.1.call-start = ((), (), s32[]{:S(2)}) async-start(), calls=%async_computation.5 | async-start | bytes 18874368 | tf_op jit(solution)/shard_map/all_gather | solution.py:74
  108.0 33.8 %copy-start.17 = (bf16[2,2048]{1,0:T(2,128)(2,1)S(1)}, bf16[2,2048]{1,0:T(2,128)(2,1)}, u32[]{:S(2)}) copy-start(bf16[2,2048]{1,0:T(2,128)(2,1)} %param.14) | copy-start | bytes 24580
  144.4 110.5 %copy-start = (pred[512,4096]{0,1:T(8,128)(4,1)}, pred[512,4096]{0,1:T(8,128)(4,1)S(1)}, u32[]{:S(2)}) copy-start(pred[512,4096]{0,1:T(8,128)(4,1)S(1)} %broadcast_compare_fusion) | copy-start | bytes 6291460
  307.7 9.6 %copy-start.21 = (f32[1,2048]{1,0:T(1,128)S(1)}, f32[1,2048]{1,0:T(1,128)}, u32[]{:S(2)}) copy-start(f32[1,2048]{1,0:T(1,128)} %get-tuple-element.26) | copy-start | bytes 24580
  369.2 24.2 %copy-start.20 = (f32[1,2048]{1,0:T(1,128)S(1)}, f32[1,2048]{1,0:T(1,128)}, u32[]{:S(2)}) copy-start(f32[1,2048]{1,0:T(1,128)} %get-tuple-element.27) | copy-start | bytes 24580
  393.4 7.9 copy-start.22
  401.3 7.2 copy-start.13
  401.3 7.2 copy-start.15
  411.4 1.0 copy-start.6
  413.9 350.6 %all-gather.10.cloned.1.call-start = ((), (), s32[]{:S(2)}) async-start(), calls=%async_computation.4 | async-start | bytes 18874368 | tf_op jit(solution)/shard_map/all_gather | solution.py:75
  414.2 10.2 %copy-start.8 = (bf16[512,16,128]{2,0,1:T(8,128)(2,1)S(1)}, bf16[512,16,128]{2,0,1:T(8,128)(2,1)}, u32[]{:S(2)}) copy-start(bf16[512,16,128]{2,0,1:T(8,128)(2,1)} %fusion.98) | copy-start | bytes 6291460
  428.6 4.8 copy-start.3
  428.6 4.8 copy-start.5
  428.6 98.4 %all-to-all-start.1 = ((bf16[2,512,16,128]{3,1,0,2:T(8,128)(2,1)}), bf16[2,512,16,128]{3,1,0,2:T(8,128)(2,1)}, u32[]{:S(2)}, u32[]{:S(2)}) async-start(bf16[2,512,16,128]{3,1,0,2:T(8,128)(2,1)} %copy.53), calls=%async_computation.1 | async-start | bytes 8388608 | tf_op jit(solution)/shard_map/all_to_all | solution.py:88
  527.0 79.9 %all-to-all-start = ((bf16[2,512,16,128]{1,3,0,2:T(8,128)(2,1)}), bf16[2,512,16,128]{1,3,0,2:T(8,128)(2,1)}, u32[]{:S(2)}, u32[]{:S(2)}) async-start(bf16[2,512,16,128]{1,3,0,2:T(8,128)(2,1)} %copy.50), calls=%async_computation | async-start | bytes 8388608 | tf_op jit(solution)/shard_map/all_to_all | solution.py:87
  644.4 2.9 copy-start.9
  644.4 2.9 copy-start.10
  662.3 10.0 %copy-start.1 = (pred[512,4096]{0,1:T(8,128)(4,1)S(1)}, pred[512,4096]{0,1:T(8,128)(4,1)}, u32[]{:S(2)}) copy-start(pred[512,4096]{0,1:T(8,128)(4,1)} %copy-done) | copy-start | bytes 6291460
  662.3 10.0 %copy-start.16 = (bf16[512,16,64]{0,2,1:T(8,128)(2,1)S(1)}, bf16[512,16,64]{0,2,1:T(8,128)(2,1)}, u32[]{:S(2)}) copy-start(bf16[512,16,64]{0,2,1:T(8,128)(2,1)} %get-tuple-element.9) | copy-start | bytes 3145732
  817.2 9.6 %copy-start.19 = (f32[1,2048]{1,0:T(1,128)S(1)}, f32[1,2048]{1,0:T(1,128)}, u32[]{:S(2)}) copy-start(f32[1,2048]{1,0:T(1,128)} %get-tuple-element.25) | copy-start | bytes 24580
Sparse Core Ops, SparseCore 0:
  78.0 84.5 all-gather.7
  164.7 81.6 all-gather.5
  414.0 131.2 all-gather.11
  546.8 106.0 all-gather.9
where the time goes:
time: 920 us; the launch traced here: 910 us
  matrix products  424 us (46%)
  waiting for transfers between devices  175 us (19%)
  local copies, waits for them, and re-layouts  145 us (16%)
  other arithmetic  119 us (13%)
  blocking collectives  21.4 us (2%)
  between operations  14.6 us (2%)
  starting transfers between devices  10.7 us (1%)
    dot_general x2, matrix products, attend(): jnp.einsum('kgts,skd->tkgd', attn_probs, value_all, preferred_element_typ...  105 us
    dot_general x2, matrix products, attend(): jnp.einsum('tkgd,skd->kgts', grouped, key_all, preferred_element_type=jnp...  102 us
    all_to_all x1, waiting for transfers between devices, per_device(): value_heads = lax.all_to_all(jnp.stack(value_list), 'cp', 2, 1, tiled=True)  89.5 us
    reduce_sum x2, other arithmetic, attend(): jnp.sum(exp_scores, axis=-1, keepdims=True)  82.1 us
    unnamed x53, local copies, waits for them, and re-layouts  76.1 us
    all_to_all x1, waiting for transfers between devices, per_device(): key_heads = lax.all_to_all(jnp.stack(key_list), 'cp', 2, 1, tiled=True)  67.2 us
    dot_general x2, matrix products, per_device(): jnp.dot(normed_mlp, w_up[layer_idx], preferred_element_type=jnp.float32)  53.4 us
    dot_general x2, matrix products, per_device(): jnp.dot(normed_mlp, w_gate[layer_idx], preferred_element_type=jnp.float32)  50.6 us
  transfers between devices with their start and end apart: 6, of which 3 were waited for; matrix products, arithmetic and copies ran while one was open for 35% of the time, Pallas kernels for 0%

commit v1 on v0

v1 whole, which is shorter than its diff:
```python
import functools

import jax
import jax.numpy as jnp
from jax import lax
from jax.experimental import pallas as pl
from jax.experimental.pallas import tpu as pltpu
from jax.sharding import PartitionSpec as P

NORM_EPS = 1e-5
ROPE_BASE = 10000.0
LOG2E = 1.4426950408889634
TK = 512


def rms_norm(values, gain_vec):
    wide_vals = values.astype(jnp.float32)
    inv_rms = lax.rsqrt(jnp.mean(wide_vals * wide_vals, axis=-1, keepdims=True) + NORM_EPS)
    return (wide_vals * inv_rms * gain_vec.astype(jnp.float32)).astype(jnp.bfloat16)


def rope_tables(pos_vec, head_dim):
    inv_freq = ROPE_BASE ** (-jnp.arange(0, head_dim, 2, dtype=jnp.float32) / head_dim)
    angles = pos_vec.astype(jnp.float32)[..., None] * inv_freq
    cos, sin = jnp.cos(angles), jnp.sin(angles)
    return jnp.concatenate([cos, cos], axis=-1), jnp.concatenate([-sin, sin], axis=-1)


def qkv_kernel(heads, dim, aliased, h_ref, w_ref, cos_ref, sin_ref, *refs):
    q_ref, k_ref, vt_ref, kc_ref, vc_ref = refs[2:] if aliased else refs
    y = jnp.dot(h_ref[...], w_ref[...], preferred_element_type=jnp.float32)
    cos, sin = cos_ref[...], sin_ref[...]
    width = heads * dim

    def rope(x):
        return x * cos + pltpu.roll(x, dim // 2, 1) * sin

    keys = []
    for n in range(heads):
        lo, hi = n * dim, (n + 1) * dim
        q_ref[:, lo:hi] = rope(y[:, lo:hi]).astype(jnp.bfloat16)
        keys.append(rope(y[:, width + lo : width + hi]))
        k_ref[:, lo:hi] = keys[n].astype(jnp.bfloat16)
    vals = y[:, 2 * width :]
    vt_ref[...] = vals.T.astype(jnp.bfloat16)
    kc_ref[0] = jnp.stack(keys, axis=1).astype(jnp.bfloat16)
    vc_ref[0] = jnp.stack([vals[:, n * dim : (n + 1) * dim] for n in range(heads)], axis=1).astype(jnp.bfloat16)


def qkv(hidden_all, weights, cos, sin, caches, cache_shape, layer, first, reverse, block):
    rows, model = hidden_all.shape
    heads, dim = cache_shape[2], cache_shape[3]
    width = heads * dim
    n = rows // block
    place = (lambda i: n - 1 - i) if reverse else (lambda i: i)
    cache = jax.ShapeDtypeStruct(cache_shape, jnp.bfloat16)
    cache_spec = pl.BlockSpec((1, block, heads, dim), lambda i: (layer, first + place(i), 0, 0))
    args = [hidden_all, weights, cos, sin]
    in_specs = [
        pl.BlockSpec((block, model), lambda i: (i, 0)),
        pl.BlockSpec((model, 3 * width), lambda i: (0, 0)),
        pl.BlockSpec((block, dim), lambda i: (first + place(i), 0)),
        pl.BlockSpec((block, dim), lambda i: (first + place(i), 0)),
    ]
    alias = {}
    if caches is not None:
        args += list(caches)
        in_specs += [pl.BlockSpec(memory_space=pl.ANY)] * 2
        alias = {4: 3, 5: 4}
    return pl.pallas_call(
        functools.partial(qkv_kernel, heads, dim, caches is not None),
        grid=(n,),
        out_shape=[
            jax.ShapeDtypeStruct((rows, width), jnp.bfloat16),
            jax.ShapeDtypeStruct((rows, width), jnp.bfloat16),
            jax.ShapeDtypeStruct((width, rows), jnp.bfloat16),
            cache,
            cache,
        ],
        in_specs=in_specs,
        out_specs=[
            pl.BlockSpec((block, width), lambda i: (place(i), 0)),
            pl.BlockSpec((block, width), lambda i: (place(i), 0)),
            pl.BlockSpec((width, block), lambda i: (0, place(i))),
            cache_spec,
            cache_spec,
        ],
        input_output_aliases=alias,
        compiler_params=pltpu.CompilerParams(vmem_limit_bytes=40 * 1024 * 1024),
        cost_estimate=pl.CostEstimate(flops=2 * rows * model * 3 * width, bytes_accessed=rows * model * 2, transcendentals=0),
    )(*args)


def attn_kernel(heads, dim, parts, q_ref, *refs):
    o_ref = refs[-1]
    kv = [(refs[2 * p], refs[2 * p + 1]) for p in range(parts)]
    tq = q_ref.shape[0]
    qb = pl.program_id(0)
    scale = LOG2E * dim**-0.5
    queries = [q_ref[:, n * dim : (n + 1) * dim] for n in range(heads)]

    def chunk(k_ref, vt_ref, start, carry, masked):
        out = []
        for n in range(heads):
            m, l, acc = carry[n]
            k = k_ref[pl.ds(start, TK), n * dim : (n + 1) * dim]
            s = lax.dot_general(k, queries[n], (((1,), (1,)), ((), ())), preferred_element_type=jnp.float32)
            if masked:
                row = start + lax.broadcasted_iota(jnp.int32, s.shape, 0)
                col = qb * tq + lax.broadcasted_iota(jnp.int32, s.shape, 1)
                s = jnp.where(row <= col, s, -jnp.inf)
            m_new = jnp.maximum(m, jnp.max(s, axis=0, keepdims=True))
            a = jnp.exp2((m - m_new) * scale)
            p = jnp.exp2((s - m_new) * scale)
            l = l * a + jnp.sum(p, axis=0, keepdims=True)
            vt = vt_ref[n * dim : (n + 1) * dim, pl.ds(start, TK)]
            acc = acc * a + jnp.dot(vt, p.astype(jnp.bfloat16), preferred_element_type=jnp.float32)
            out.append((m_new, l, acc))
        return tuple(out)

    carry = tuple(
        (jnp.full((1, tq), -jnp.inf, jnp.float32), jnp.zeros((1, tq), jnp.float32), jnp.zeros((dim, tq), jnp.float32))
        for _ in range(heads)
    )
    if parts == 2:
        k_ref, vt_ref = kv[0]
        carry = lax.fori_loop(
            0, k_ref.shape[0] // TK, lambda j, c: chunk(k_ref, vt_ref, pl.multiple_of(j * TK, TK), c, False), carry
        )
    k_last, vt_last = kv[-1]
    full = (qb * tq) // TK
    carry = lax.fori_loop(0, full, lambda j, c: chunk(k_last, vt_last, pl.multiple_of(j * TK, TK), c, False), carry)
    carry = chunk(k_last, vt_last, pl.multiple_of(full * TK, TK), carry, True)
    for n in range(heads):
        m, l, acc = carry[n]
        o_ref[:, n * dim : (n + 1) * dim] = (acc / l).T.astype(jnp.bfloat16)


def attention(q, kv, heads, dim, block, reverse):
    rows, width = q.shape
    n = rows // block
    place = (lambda i: n - 1 - i) if reverse else (lambda i: i)
    args = [q]
    in_specs = [pl.BlockSpec((block, width), lambda i: (i, 0))]
    for k, vt in kv:
        args += [k, vt]
        in_specs += [pl.BlockSpec(k.shape, lambda i: (0, 0)), pl.BlockSpec(vt.shape, lambda i: (0, 0))]
    pairs = rows * rows * (2 * len(kv) - 1) // 2
    return pl.pallas_call(
        functools.partial(attn_kernel, heads, dim, len(kv)),
        grid=(n,),
        out_shape=jax.ShapeDtypeStruct((rows, width), jnp.bfloat16),
        in_specs=in_specs,
        out_specs=pl.BlockSpec((block, width), lambda i: (place(i), 0)),
        compiler_params=pltpu.CompilerParams(vmem_limit_bytes=40 * 1024 * 1024),
        cost_estimate=pl.CostEstimate(flops=4 * pairs * width, bytes_accessed=rows * width * 8, transcendentals=pairs * heads),
    )(*args)


def solution(mesh):
    cp_size = mesh.shape["cp"]
    row_spec = P(("req", "cp"), None)
    pos_spec = P(("req", "cp"))
    rep_spec = P()
    cache_spec = P(None, "req", "cp", None)

    def per_device(hidden, positions, gain_attn, gain_mlp, w_query, w_key, w_value, w_out, w_gate, w_up, w_down):
        num_layers, model, all_heads, dim = w_query.shape
        heads = all_heads // cp_size
        width = heads * dim
        rows = hidden.shape[0]
        block = rows // 2
        half = cp_size * block
        cache_shape = (num_layers, 2 * half, heads, dim)
        me = lax.axis_index("cp")

        def mine(w):
            return lax.dynamic_slice_in_dim(w, me * heads, heads, 2).reshape(num_layers, model, width)

        w_all = jnp.concatenate([mine(w_query), mine(w_key), mine(w_value)], axis=2)
        pos_all = lax.all_gather(positions, "cp", tiled=False)
        hidden, pos_all = lax.optimization_barrier((hidden, pos_all))
        pos_nat = jnp.concatenate([pos_all[:, :block].reshape(-1), pos_all[::-1, block:].reshape(-1)])
        cos, sin = rope_tables(pos_nat, dim)
        caches = None
        for layer in range(num_layers):
            normed = rms_norm(hidden, gain_attn[layer])
            h_a = lax.all_gather(normed[:block], "cp", tiled=True)
            h_b = lax.all_gather(normed[block:], "cp", tiled=True)
            q_a, k_a, vt_a, *caches = qkv(h_a, w_all[layer], cos, sin, caches, cache_shape, layer, 0, False, block)
            o_a = attention(q_a, [(k_a, vt_a)], heads, dim, block, False)
            o_a = lax.all_to_all(o_a, "cp", 0, 1, tiled=True)
            q_b, k_b, vt_b, *caches = qkv(h_b, w_all[layer], cos, sin, caches, cache_shape, layer, cp_size, True, block)
            o_b = attention(q_b, [(k_a, vt_a), (k_b, vt_b)], heads, dim, block, True)
            o_b = lax.all_to_all(o_b, "cp", 0, 1, tiled=True)
            attn_out = jnp.concatenate([o_a, o_b], axis=0)
            attn_proj = jnp.dot(attn_out, w_out[layer].reshape(all_heads * dim, model), preferred_element_type=jnp.float32)
            hidden = (hidden.astype(jnp.float32) + attn_proj).astype(jnp.bfloat16)
            normed_mlp = rms_norm(hidden, gain_mlp[layer])
            gate_act = jnp.dot(normed_mlp, w_gate[layer], preferred_element_type=jnp.float32)
            up_act = jnp.dot(normed_mlp, w_up[layer], preferred_element_type=jnp.float32)
            mlp_hidden = (jax.nn.silu(gate_act) * up_act).astype(jnp.bfloat16)
            mlp_out = jnp.dot(mlp_hidden, w_down[layer], preferred_element_type=jnp.float32)
            hidden = (hidden.astype(jnp.float32) + mlp_out).astype(jnp.bfloat16)
        return hidden, caches[0], caches[1]

    in_specs = (row_spec, pos_spec) + (rep_spec,) * 9
    return jax.shard_map(per_device, mesh=mesh, in_specs=in_specs, out_specs=(row_spec, cache_spec, cache_spec), check_vma=False)
```

time: 920 us -> 661 us (0.72)
  matrix products: 424 us -> 172 us
  Pallas kernels: 0 us -> 204 us
  other arithmetic: 119 us -> 20.2 us
  waiting for transfers between devices: 175 us -> 101 us
  local copies, waits for them, and re-layouts: 145 us -> 85.3 us
  blocking collectives: 21.4 us -> 38.7 us
    dot_general x14 -> x8, matrix products: 397 us -> 172 us  [the longest x2 54.4 us: per_device(): jnp.dot(normed_mlp, w_up[layer], preferred_element_type=jnp.float32)]
    pallas_call x0 -> x8, Pallas kernels: none -> 204 us  [the longest x4 149 us: attention(): pl.pallas_call(functools.partial(attn_kernel, heads, dim, len(kv)), grid=...]
    all_to_all x2 -> x3, waiting for transfers between devices: 157 us -> 2.75 us  [the longest x1 2.75 us: per_device(): o_a = lax.all_to_all(o_a, 'cp', 0, 1, tiled=True)]
    reduce_sum x2 -> x0, other arithmetic: 82.1 us -> none  [attend(): jnp.sum(exp_scores, axis=-1, keepdims=True)]
    all_gather x4, waiting for transfers between devices: 18.3 us -> 97.2 us  [the longest x2 52 us: per_device(): h_b = lax.all_gather(normed[block:], 'cp', tiled=True)]
    unnamed x53 -> x61, local copies, waits for them, and re-layouts: 76.1 us -> 39.3 us
    slice x5 -> x3, local copies, waits for them, and re-layouts: 48.2 us -> 15 us  [the longest x1 12 us: per_device(): w_out[layer].reshape(all_heads * dim, model)]
    unnamed x4 -> x0, matrix products: 27.1 us -> none
  transfers between devices with their start and end apart: 6 -> 7, of which waited for: 3 -> 4; matrix products, arithmetic and copies ran while one was open for 35% -> 11% of each run, Pallas kernels for 0% -> 11%
where the time goes in v1:
time: 661 us; the launch traced here: 650 us
  Pallas kernels  204 us (31%)
  matrix products  172 us (26%)
  waiting for transfers between devices  101 us (15%)
  local copies, waits for them, and re-layouts  85.3 us (13%)
  blocking collectives  38.7 us (6%)
  other arithmetic  20.2 us (3%)
  between operations  14.5 us (2%)
  starting transfers between devices  13.9 us (2%)
    pallas_call x4, Pallas kernels, attention(): pl.pallas_call(functools.partial(attn_kernel, heads, dim, len(kv)), grid=...  149 us
    pallas_call x4, Pallas kernels, qkv(): pl.pallas_call(functools.partial(qkv_kernel, heads, dim, caches is not No...  54.8 us
    dot_general x2, matrix products, per_device(): jnp.dot(normed_mlp, w_up[layer], preferred_element_type=jnp.float32)  54.4 us
    all_gather x2, waiting for transfers between devices, per_device(): h_b = lax.all_gather(normed[block:], 'cp', tiled=True)  52 us
    dot_general x2, matrix products, per_device(): jnp.dot(normed_mlp, w_gate[layer], preferred_element_type=jnp.float32)  50.5 us
    dot_general x2, matrix products, per_device(): jnp.dot(mlp_hidden, w_down[layer], preferred_element_type=jnp.float32)  48.9 us
    all_gather x2, waiting for transfers between devices, per_device(): h_a = lax.all_gather(normed[:block], 'cp', tiled=True)  45.3 us
    unnamed x61, local copies, waits for them, and re-layouts  39.3 us
  transfers between devices with their start and end apart: 7, of which 4 were waited for; matrix products, arithmetic and copies ran while one was open for 11% of the time, Pallas kernels for 11%

profile of v1, /device:TPU:113, one launch (start us, length us, event | category | flops | bytes accessed | tf_op | source)
XLA Modules:
  0.0 649.9 jit_solution(101653034262611635)
XLA Ops:
  7.2 18.9 %all-gather.1 = s32[8,1,512]{2,1,0:T(1,128)S(1)} all-gather(s32[1,1,512]{2,1,0:T(1,128)} %bitcast.115), channel_id=2, replica_groups=mesh['req'=2,'cp'=8] {'cp'}, dimensions={0}, use_global_device_ids=true | all-gather | bytes 18432 | tf_op jit(solution)/shard_map/all_gather | solution.py:181
  26.1 2.1 fusion.28
  29.6 2.1 fusion.30
  34.2 6.2 constant_dynamic-slice_fusion.2
  40.4 4.7 copy.41
  45.1 2.5 copy.33
  47.6 9.7 %constant_dynamic-slice_fusion = (bf16[2,2048,2,128]{3,2,1,0:T(2,128)(2,1)}, bf16[2,2048,2,128]{3,2,1,0:T(2,128)(2,1)}) fusion(bf16[2,2048,16,128]{3,2,1,0:T(8,128)(2,1)} %param.17, s32[]{:T(128)S(6)} %select_n.2, bf16[2,2048,16,128]{3,2,1,0:T(8,128)(2,1)} %param.16), kind=kLoop, calls=%fused_computation.79 | loop fusion | bytes 8388612 | tf_op jit(solution)/shard_map/dynamic_slice | solution.py:178
  57.3 4.7 copy.43
  62.0 2.5 copy.35
  64.5 4.7 copy.42
  69.3 2.5 copy.34
  71.8 3.5 pad_maximum_fusion
  75.3 7.5 %fusion.70 = (f32[4096,64]{1,0:T(8,128)S(1)}, f32[4096,64]{1,0:T(8,128)S(1)}, f32[4096,64]{1,0:T(8,128)S(1)}) fusion(f32[64]{0:T(128)S(1)} %multiply_power_fusion, f32[4096]{0:T(1024)S(1)} %add_convert_fusion), kind=kLoop, calls=%fused_computation.67 | loop fusion | flops 524288 | bytes 3162368 | tf_op jit(solution)/shard_map/neg | solution.py:26
  82.8 2.5 pad_maximum_fusion.1
  85.2 3.0 slice_bitcast_fusion
  88.2 1.6 copy-done
  89.8 1.9 copy-done.6
  91.7 13.5 %shard_map.130 = (bf16[2048,256]{1,0:T(8,128)(2,1)S(1)}, bf16[2048,256]{1,0:T(8,128)(2,1)S(1)}, bf16[256,2048]{1,0:T(8,128)(2,1)S(1)}, bf16[2,4096,2,128]{3,2,1,0:T(2,128)(2,1)}, bf16[2,4096,2,128]{3,2,1,0:T(2,128)(2,1)}) custom-call(bf16[2048,2048]{1,0:T(8,128)(2,1)} %all-gather.7.cloned.1.call-done.h_ref, bf16[2048,768]{1,0:T(8,128)(2,1)S(1)} %copy-done.6, ...), custom_call_target="tpu_custom_call" | custom-call | flops 6442450944 | bytes 8388608 | tf_op jit(solution)/shard_map/pallas_call | solution.py:70
  108.2 24.0 %all-gather.9.cloned.1.call-done.h_ref = bf16[2048,2048]{1,0:T(8,128)(2,1)} async-done(((bf16[256,2048]{1,0:T(8,128)(2,1)}), bf16[2048,2048]{1,0:T(8,128)(2,1)}) %all-gather.9.cloned.1.call-update) | async-done | bytes 8388624 | tf_op jit(solution)/shard_map/all_gather | solution.py:189
  132.3 1.6 copy-done.1
  133.9 1.9 copy-done.7
  135.8 13.8 %shard_map.132 = (bf16[2048,256]{1,0:T(8,128)(2,1)S(1)}, bf16[2048,256]{1,0:T(8,128)(2,1)S(1)}, bf16[256,2048]{1,0:T(8,128)(2,1)S(1)}, bf16[2,4096,2,128]{3,2,1,0:T(2,128)(2,1)}, bf16[2,4096,2,128]{3,2,1,0:T(2,128)(2,1)}) custom-call(bf16[2048,2048]{1,0:T(8,128)(2,1)} %all-gather.9.cloned.1.call-done.h_ref, ...), custom_call_target="tpu_custom_call", output_to_operand_aliasing={{3}: (4, {}), {4}: (5, {})} | custom-call | flops 6442450944 | bytes 8388608 | tf_op jit(solution)/shard_map/pallas_call | solution.py:70
  149.5 53.7 %shard_map.133 = bf16[2048,256]{1,0:T(8,128)(2,1)S(1)} custom-call(bf16[2048,256]{1,0:T(8,128)(2,1)S(1)} %get-tuple-element.32.q_ref, bf16[2048,256]{1,0:T(8,128)(2,1)S(1)} %copy-done.17, bf16[256,2048]{1,0:T(8,128)(2,1)S(1)} %copy-done.20, bf16[2048,256]{1,0:T(8,128)(2,1)S(1)} %get-tuple-element.33.refs_2_, bf16[256,2048]{1,0:T(8,128)(2,1)S(1)} %get-tuple-element.34.refs_3_), custom_call_target="tpu_custom_call" | custom-call | flops 6442450944 | bytes 4194304 | tf_op jit(solution)/shard_map/pallas_call | solution.py:149
  204.6 4.4 all-to-all-start.1
  213.2 20.8 %shard_map.131 = bf16[2048,256]{1,0:T(8,128)(2,1)S(1)} custom-call(bf16[2048,256]{1,0:T(8,128)(2,1)S(1)} %copy-done.15, bf16[2048,256]{1,0:T(8,128)(2,1)S(1)} %copy-done.18, bf16[256,2048]{1,0:T(8,128)(2,1)S(1)} %copy-done.21), custom_call_target="tpu_custom_call" | custom-call | flops 2147483648 | bytes 4194304 | tf_op jit(solution)/shard_map/pallas_call | solution.py:149
  235.4 4.9 all-to-all-start
  240.3 12.0 %fusion.75 = (bf16[1,16,128,2048]{3,2,1,0:T(8,128)(2,1)}, bf16[1,16,128,2048]{3,2,1,0:T(8,128)(2,1)}) fusion(bf16[2,16,128,2048]{3,2,1,0:T(8,128)(2,1)} %param.18), kind=kLoop, calls=%fused_computation.87 | loop fusion | bytes 33554432 | tf_op jit(solution)/shard_map/slice | solution.py:197
  252.3 2.7 all-to-all-done
  255.0 9.3 %fusion.32 = (f32[512]{0:T(512)S(1)}, bf16[512,2048]{1,0:T(8,128)(2,1)S(1)}) fusion(bf16[2048,2048]{1,0:T(8,128)(2,1)} %bitcast.102, bf16[256,2048]{0,1:T(8,128)(2,1)} %bitcast.11, bf16[256,2048]{0,1:T(8,128)(2,1)S(1)} %bitcast.103, bf16[512,2048]{1,0:T(8,128)(2,1)} %param.11), kind=kOutput, calls=%fused_computation.39 | convolution fusion | flops 4305452544 | bytes 14682112 | tf_op jit(solution)/shard_map/dot_general | solution.py:197
  265.6 25.3 %fusion.10 = f32[512,8192]{1,0:T(8,128)} fusion(bf16[2,2048,8192]{2,1,0:T(8,128)(2,1)} %param.19, bf16[512,2048]{1,0:T(8,128)(2,1)S(1)} %get-tuple-element.65, f32[2048]{0:T(1024)S(1)} %bitcast.113, f32[512]{0:T(512)S(1)} %add_rsqrt_fusion.2), kind=kOutput, calls=%fused_computation.10 | convolution fusion | flops 17184063488 | bytes 52439040 | tf_op jit(solution)/shard_map/dot_general | solution.py:200
  290.8 27.6 %multiply_convert_fusion.1.clone.3.clone.5 = bf16[512,8192]{1,0:T(8,128)(2,1)} fusion(f32[512,8192]{1,0:T(8,128)} %fusion.10, bf16[2,2048,8192]{2,1,0:T(8,128)(2,1)} %param.20, bf16[512,2048]{1,0:T(8,128)(2,1)} %copy-done.26, f32[2048]{0:T(1024)S(1)} %bitcast.114, f32[512]{0:T(512)S(1)} %add_rsqrt_fusion.2), kind=kOutput, calls=%fused_computation.19.clone.clone.clone.clone.clone.clone.clone.2 | convolution fusion | flops 17209229312 | bytes 60827648 | tf_op jit(solution)/shard_map/dot_general | solution.py:201
  318.4 24.3 %fusion.36 = (f32[512]{0:T(512)S(1)}, bf16[512,2048]{1,0:T(8,128)(2,1)S(1)}) fusion(bf16[2,8192,2048]{2,1,0:T(8,128)(2,1)} %param.21, bf16[512,2048]{1,0:T(8,128)(2,1)} %copy-done.26, bf16[512,8192]{1,0:T(8,128)(2,1)} %multiply_convert_fusion.1.clone.3.clone.5), kind=kOutput, calls=%fused_computation.43 | convolution fusion | flops 17186160640 | bytes 46139392 | tf_op jit(solution)/shard_map/dot_general | solution.py:203
  345.6 45.3 %all-gather.11.cloned.1.call-done.h_ref = bf16[2048,2048]{1,0:T(8,128)(2,1)} async-done(((bf16[256,2048]{1,0:T(8,128)(2,1)}), bf16[2048,2048]{1,0:T(8,128)(2,1)}) %all-gather.11.cloned.1.call-update) | async-done | bytes 8388624 | tf_op jit(solution)/shard_map/all_gather | solution.py:188
  390.9 1.6 copy-done.2
  392.5 1.9 copy-done.4
  394.3 13.7 %shard_map.134 = (bf16[2048,256]{1,0:T(8,128)(2,1)S(1)}, bf16[2048,256]{1,0:T(8,128)(2,1)S(1)}, bf16[256,2048]{1,0:T(8,128)(2,1)S(1)}, bf16[2,4096,2,128]{3,2,1,0:T(2,128)(2,1)}, bf16[2,4096,2,128]{3,2,1,0:T(2,128)(2,1)}) custom-call(bf16[2048,2048]{1,0:T(8,128)(2,1)} %all-gather.11.cloned.1.call-done.h_ref, ...), custom_call_target="tpu_custom_call", output_to_operand_aliasing={{3}: (4, {}), {4}: (5, {})} | custom-call | flops 6442450944 | bytes 8388608 | tf_op jit(solution)/shard_map/pallas_call | solution.py:70
  410.1 27.9 %all-gather.13.cloned.1.call-done.h_ref = bf16[2048,2048]{1,0:T(8,128)(2,1)} async-done(((bf16[256,2048]{1,0:T(8,128)(2,1)}), bf16[2048,2048]{1,0:T(8,128)(2,1)}) %all-gather.13.cloned.1.call-update) | async-done | bytes 8388624 | tf_op jit(solution)/shard_map/all_gather | solution.py:189
  438.0 1.6 copy-done.3
  439.6 1.9 copy-done.5
  441.5 13.8 %shard_map.136 = (bf16[2048,256]{1,0:T(8,128)(2,1)S(1)}, bf16[2048,256]{1,0:T(8,128)(2,1)S(1)}, bf16[256,2048]{1,0:T(8,128)(2,1)S(1)}, bf16[2,4096,2,128]{3,2,1,0:T(2,128)(2,1)}, bf16[2,4096,2,128]{3,2,1,0:T(2,128)(2,1)}) custom-call(bf16[2048,2048]{1,0:T(8,128)(2,1)} %all-gather.13.cloned.1.call-done.h_ref, ...), custom_call_target="tpu_custom_call", output_to_operand_aliasing={{3}: (4, {}), {4}: (5, {})} | custom-call | flops 6442450944 | bytes 8388608 | tf_op jit(solution)/shard_map/pallas_call | solution.py:70
  455.3 53.5 %shard_map.137 = bf16[2048,256]{1,0:T(8,128)(2,1)S(1)} custom-call(bf16[2048,256]{1,0:T(8,128)(2,1)S(1)} %get-tuple-element.42.q_ref, bf16[2048,256]{1,0:T(8,128)(2,1)S(1)} %copy-done.9, bf16[256,2048]{1,0:T(8,128)(2,1)S(1)} %copy-done.12, bf16[2048,256]{1,0:T(8,128)(2,1)S(1)} %get-tuple-element.43.refs_2_, bf16[256,2048]{1,0:T(8,128)(2,1)S(1)} %get-tuple-element.44.refs_3_), custom_call_target="tpu_custom_call" | custom-call | flops 6442450944 | bytes 4194304 | tf_op jit(solution)/shard_map/pallas_call | solution.py:149
  510.1 4.4 all-to-all-start.3
  515.7 20.8 %shard_map.135 = bf16[2048,256]{1,0:T(8,128)(2,1)S(1)} custom-call(bf16[2048,256]{1,0:T(8,128)(2,1)S(1)} %get-tuple-element.37.q_ref, bf16[2048,256]{1,0:T(8,128)(2,1)S(1)} %copy-done.10, bf16[256,2048]{1,0:T(8,128)(2,1)S(1)} %copy-done.13), custom_call_target="tpu_custom_call" | custom-call | flops 2147483648 | bytes 4194304 | tf_op jit(solution)/shard_map/pallas_call | solution.py:149
  537.1 19.8 %all_to_all.76 = bf16[8,256,256]{1,2,0:T(8,128)(2,1)S(1)} all-to-all(bf16[8,256,256]{1,2,0:T(8,128)(2,1)S(1)} %copy.38), channel_id=1, replica_groups=mesh['req'=2,'cp'=8] {'cp'}, dimensions={0} | all-to-all | bytes 2097152 | tf_op jit(solution)/shard_map/all_to_all | solution.py:192
  556.9 9.3 %fusion.40 = (f32[512]{0:T(512)S(1)}, bf16[512,2048]{1,0:T(8,128)(2,1)S(1)}) fusion(bf16[2048,2048]{1,0:T(8,128)(2,1)} %bitcast.101, bf16[256,2048]{0,1:T(8,128)(2,1)} %bitcast.24, bf16[256,2048]{0,1:T(8,128)(2,1)S(1)} %bitcast.104, bf16[512,2048]{1,0:T(8,128)(2,1)} %copy-done.22), kind=kOutput, calls=%fused_computation.47 | convolution fusion | flops 4305452544 | bytes 14682112 | tf_op jit(solution)/shard_map/dot_general | solution.py:197
  566.2 25.3 %fusion.4 = f32[512,8192]{1,0:T(8,128)} fusion(bf16[2,2048,8192]{2,1,0:T(8,128)(2,1)} %param.19, bf16[512,2048]{1,0:T(8,128)(2,1)S(1)} %get-tuple-element.69, f32[2048]{0:T(1024)S(1)} %bitcast.111, f32[512]{0:T(512)S(1)} %add_rsqrt_fusion), kind=kOutput, calls=%fused_computation.4 | convolution fusion | flops 17184063488 | bytes 52439040 | tf_op jit(solution)/shard_map/dot_general | solution.py:200
  591.5 26.9 %multiply_convert_fusion.clone.7 = bf16[512,8192]{1,0:T(8,128)(2,1)} fusion(f32[512,8192]{1,0:T(8,128)} %fusion.4, bf16[2,2048,8192]{2,1,0:T(8,128)(2,1)} %param.20, bf16[512,2048]{1,0:T(8,128)(2,1)S(1)} %get-tuple-element.69, f32[2048]{0:T(1024)S(1)} %bitcast.112, f32[512]{0:T(512)S(1)} %add_rsqrt_fusion), kind=kOutput, calls=%fused_computation.18.clone.clone.clone.clone.clone.2 | convolution fusion | flops 17209229312 | bytes 60827648 | tf_op jit(solution)/shard_map/dot_general | solution.py:201
  618.3 24.6 %fusion.43 = bf16[512,2048]{1,0:T(8,128)(2,1)} fusion(bf16[512,2048]{1,0:T(8,128)(2,1)S(1)} %get-tuple-element.69, bf16[2,8192,2048]{2,1,0:T(8,128)(2,1)} %param.21, bf16[512,8192]{1,0:T(8,128)(2,1)} %multiply_convert_fusion.clone.7), kind=kOutput, calls=%fused_computation.50 | convolution fusion | flops 17183014912 | bytes 46137344 | tf_op jit(solution)/shard_map/dot_general | solution.py:203
  (77 shorter events, 23.0 us)
Async XLA Ops:
  7.2 81.0 %all-gather.7.cloned.1.call-start = ((), (), s32[]{:S(2)}) async-start(), calls=%async_computation.4 | async-start | bytes 9437184 | tf_op jit(solution)/shard_map/all_gather | solution.py:188
  33.3 99.0 %all-gather.9.cloned.1.call-start = ((), (), s32[]{:S(2)}) async-start(), calls=%async_computation.5 | async-start | bytes 9437184 | tf_op jit(solution)/shard_map/all_gather | solution.py:189
  88.2 1.6 copy-start
  89.8 1.9 copy-start.6
  105.3 1.0 copy-start.14
  106.3 1.0 copy-start.16
  107.3 1.0 copy-start.19
  132.3 1.6 copy-start.1
  133.9 1.9 copy-start.7
  135.8 13.8 %copy-start.17 = (bf16[2048,256]{1,0:T(8,128)(2,1)S(1)}, bf16[2048,256]{1,0:T(8,128)(2,1)}, u32[]{:S(2)}) copy-start(bf16[2048,256]{1,0:T(8,128)(2,1)} %copy-done.16) | copy-start | bytes 3145732
  135.8 13.8 %copy-start.20 = (bf16[256,2048]{1,0:T(8,128)(2,1)S(1)}, bf16[256,2048]{1,0:T(8,128)(2,1)}, u32[]{:S(2)}) copy-start(bf16[256,2048]{1,0:T(8,128)(2,1)} %copy-done.19) | copy-start | bytes 3145732
  203.2 5.7 copy-start.24
  204.6 30.8 %all-to-all-start.1 = ((bf16[8,256,256]{1,2,0:T(8,128)(2,1)}), bf16[8,256,256]{1,2,0:T(8,128)(2,1)}, u32[]{:S(2)}, u32[]{:S(2)}) async-start(bf16[8,256,256]{1,2,0:T(8,128)(2,1)} %copy.37), calls=%async_computation.1 | async-start | bytes 2097152 | tf_op jit(solution)/shard_map/all_to_all | solution.py:195
  209.6 1.2 copy-start.15
  210.8 1.2 copy-start.18
  212.0 1.2 copy-start.21
  235.4 19.6 %all-to-all-start = ((bf16[8,256,256]{1,2,0:T(8,128)(2,1)}), bf16[8,256,256]{1,2,0:T(8,128)(2,1)S(1)}, u32[]{:S(2)}, u32[]{:S(2)}) async-start(bf16[8,256,256]{1,2,0:T(8,128)(2,1)} %copy.36), calls=%async_computation | async-start | bytes 2097152 | tf_op jit(solution)/shard_map/all_to_all | solution.py:192
  240.3 150.6 %all-gather.11.cloned.1.call-start = ((), (), s32[]{:S(2)}) async-start(), calls=%async_computation.6 | async-start | bytes 9437184 | tf_op jit(solution)/shard_map/all_gather | solution.py:188
  264.3 1.3 copy-start.26
  318.4 24.3 %copy-start.23 = (f32[1,2048]{1,0:T(1,128)S(1)}, f32[1,2048]{1,0:T(1,128)}, u32[]{:S(2)}) copy-start(f32[1,2048]{1,0:T(1,128)} %get-tuple-element.62) | copy-start | bytes 24580
  342.8 2.1 copy-start.22
  345.0 93.0 %all-gather.13.cloned.1.call-start = ((), (), s32[]{:S(2)}) async-start(), calls=%async_computation.7 | async-start | bytes 9437184 | tf_op jit(solution)/shard_map/all_gather | solution.py:189
  390.9 1.6 copy-start.2
  392.5 1.9 copy-start.4
  408.1 1.0 copy-start.8
  409.1 1.0 copy-start.11
  438.0 1.6 copy-start.3
  439.6 1.9 copy-start.5
  441.5 13.8 %copy-start.9 = (bf16[2048,256]{1,0:T(8,128)(2,1)S(1)}, bf16[2048,256]{1,0:T(8,128)(2,1)}, u32[]{:S(2)}) copy-start(bf16[2048,256]{1,0:T(8,128)(2,1)} %copy-done.8) | copy-start | bytes 3145732
  441.5 13.8 %copy-start.12 = (bf16[256,2048]{1,0:T(8,128)(2,1)S(1)}, bf16[256,2048]{1,0:T(8,128)(2,1)}, u32[]{:S(2)}) copy-start(bf16[256,2048]{1,0:T(8,128)(2,1)} %copy-done.11) | copy-start | bytes 3145732
  508.7 5.7 copy-start.10
  510.1 27.0 %all-to-all-start.3 = ((bf16[8,256,256]{1,2,0:T(8,128)(2,1)}), bf16[8,256,256]{1,2,0:T(8,128)(2,1)}, u32[]{:S(2)}, u32[]{:S(2)}) async-start(bf16[8,256,256]{1,2,0:T(8,128)(2,1)} %copy.39), calls=%async_computation.3 | async-start | bytes 2097152 | tf_op jit(solution)/shard_map/all_to_all | solution.py:195
  514.5 1.2 copy-start.13
  556.9 9.3 %copy-start.25 = (f32[1,2048]{1,0:T(1,128)S(1)}, f32[1,2048]{1,0:T(1,128)}, u32[]{:S(2)}) copy-start(f32[1,2048]{1,0:T(1,128)} %get-tuple-element.60) | copy-start | bytes 24580
Sparse Core Ops, SparseCore 0:
  33.4 51.5 all-gather.6
  86.6 45.6 all-gather.8
  345.1 45.7 all-gather.10
  392.3 45.6 all-gather.12
